TPU v7x, 256 devices: a whole 4x4x8 slice. The times are simulated.
256 devices in a mesh: gx: 8 (over y, core), gy: 8 (over x, z_hi), gz: 4 (over z_lo).
Axes of the slice: x: 4, y: 4, z: 8 (z_hi: 2, z_lo: 4; z = z_hi * 4 + z_lo), core: 2. Of those that a mesh axis runs over, the one named last changes fastest.
Arguments:
- rhs: float32 [3, 128, 256, 512], P(None, 'gx', 'gy', 'gz'), may hold values from -6 to 6
- viscous: float32 [8, 16, 32], P('gx', 'gy', 'gz'), may hold values from 0.3 to 3
- reaction: float32 [8, 16, 32], P('gx', 'gy', 'gz'), may hold values from 0.05 to 1
Outputs:
- correction: float32 [3, 128, 256, 512], P(None, 'gx', 'gy', 'gz')
All inputs are finite; a program needn't handle non-finite values.
Results may differ from a plain program's by a relative error of at most 0.00008.
Values sent between devices are 32-bit elements; how exact they have to be, the bound alone decides.
A program may use at most 64 MiB of HBM per device.

v0:
```python
import functools

import jax
import jax.numpy as jnp
import numpy as np
from jax import lax
from jax.experimental import pallas as pl
from jax.experimental.pallas import tpu as pltpu
from jax.sharding import PartitionSpec as P

EDGE = 16
SPAN = EDGE + 2
HALF = 168
RING = 40
LOW, HIGH = 56, 60
MESH = pl.DeviceIdType.MESH
NN = (((1,), (0,)), ((), ()))
DIRS = [
    (dx, dy, dz)
    for dz in (0, -1, 1)
    for dy in (0, -1, 1)
    for dx in (0, -1, 1)
    if (dx, dy, dz) != (0, 0, 0)
]
FACES = [d for d in DIRS if sum(map(abs, d)) == 1]
Y_FIRST, Y_MID, Y_LAST, X_FIRST, X_LAST = 0, 16, 48, 64, 96


def table_halves(x):
    x = x.astype(np.float32)
    hi = x.astype(jnp.bfloat16)
    return hi, (x - hi.astype(np.float32)).astype(jnp.bfloat16)


def constants():
    i = np.arange(SPAN)
    basis = np.sqrt(2.0 / (SPAN + 1)) * np.sin(np.pi * np.outer(i + 1, i + 1) / (SPAN + 1))
    lam = 2.0 - 2.0 * np.cos(np.pi * (i + 1) / (SPAN + 1))
    q = np.arange(144)
    lanes = np.concatenate([np.arange(128), np.tile(np.arange(128, 144), 3)])
    forward = np.zeros((128, 256))
    back = np.zeros((144, 128))
    for h in range(8):
        for z in range(128):
            w = z - EDGE * h + 1
            if 0 <= w < SPAN:
                for n, k in enumerate(lanes):
                    if k // SPAN == h:
                        forward[z, n] = basis[w, k % SPAN]
            if 1 <= w <= EDGE:
                back[h * SPAN : (h + 1) * SPAN, z] = basis[w]
    forward[0, 128 + LOW] = 1.0
    forward[127, 128 + HIGH] = 1.0
    wide = np.zeros((144, 256))
    wide[:, :128] = back
    wide[:, 128 + LOW] = 2.0 * back[:, 0]
    wide[:, 128 + HIGH] = 2.0 * back[:, 127]
    fh, fl = table_halves(forward)
    bh, bl = table_halves(wide)
    z_forward = np.concatenate([fh, fh, fl], axis=0)
    z_back = np.concatenate(
        [bh[:128], bh[:128], bl[:128], bh[128:], bh[128:], bl[128:], np.zeros((80, 256), bh.dtype)], axis=0
    )
    into, out_of, lam_xy = [], [], []
    for parity in range(2):
        mode = np.arange(162)
        a, b = 2 * (mode // SPAN) + parity, mode % SPAN
        point = lambda x, y: basis[x, a] * basis[y, b]
        main = np.zeros((176, 128))
        for x in range(8):
            for y in range(16):
                main[:162, 16 * x + y] = point(x + 1, y + 1)
        ring = np.zeros((176, RING))
        for y in range(16):
            ring[:162, y] = point(0, y + 1)
        for x in range(8):
            ring[:162, 16 + x] = point(x + 1, 0)
            ring[:162, 24 + x] = point(x + 1, 17)
        ring[:162, 32], ring[:162, 33] = point(0, 0), point(0, 17)
        mh, ml = table_halves(main)
        rh, rl = table_halves(ring)
        into.append(np.concatenate([mh, mh, ml, rh, rh, rl, np.zeros((176, 8), mh.dtype)], axis=1))
        th, tl = mh[:HALF].T, ml[:HALF].T
        out_of.append(np.concatenate([th, th, tl, np.zeros((128, 8), mh.dtype)], axis=1))
        col = np.zeros((HALF, 1))
        col[:162, 0] = lam[a] + lam[b]
        lam_xy.append(np.repeat(col, 128, 1))
    rows = np.zeros((8, 256))
    for n, k in enumerate(lanes):
        if k < SPAN:
            rows[0, n], rows[2, n] = basis[0, k], basis[1, k]
        if k >= 7 * SPAN:
            rows[1, n], rows[3, n] = basis[17, k % SPAN], basis[16, k % SPAN]
        rows[4, n] = lam[k % SPAN]
    f32 = functools.partial(np.asarray, dtype=np.float32)
    return z_forward, np.stack(into), np.stack(out_of), z_back, f32(rows), f32(np.stack(lam_xy))


def dot(a, b):
    return lax.dot_general(a, b, NN, preferred_element_type=jnp.float32)


def halves(x):
    hi = x.astype(jnp.bfloat16)
    return hi, (x - hi.astype(jnp.float32)).astype(jnp.bfloat16)


def wide_halves(x):
    hi = x.astype(jnp.bfloat16).astype(jnp.float32)
    return hi, x - hi


def kernel(
    sizes, rhs_hbm, visc_hbm, reac_hbm, zf_hbm, into_hbm, outof_hbm, zb_hbm, row_hbm, lam_hbm,
    out_ref,
    rhs, first, resid, face, corner, zsend, zedge, rx, ry, rc, rz, re,
    part_hi, part_lo, part_end, ring, ring_end, inv, visc_plane, coef_plane,
    zf, into, outof, zb, row, lam, visc_ref, reac_ref, load_sem, send_sem, recv_sem,
):
    me = tuple(lax.axis_index(a) for a in ("gx", "gy", "gz"))

    def exists(d):
        ok = None
        for p, n, s in zip(me, sizes, d):
            if s:
                c = (p + s >= 0) & (p + s < n)
                ok = c if ok is None else ok & c
        return ok

    def peer(d):
        return tuple(p + s for p, s in zip(me, d))

    def minus(d):
        return tuple(-s for s in d)

    barrier = pltpu.get_barrier_semaphore()
    count = jnp.int32(0)
    for d in DIRS:
        ok = exists(d)
        count = count + ok.astype(jnp.int32)

        @pl.when(ok)
        def _(d=d):
            pl.semaphore_signal(barrier, inc=1, device_id=peer(d), device_id_type=MESH)

    loads = []
    pairs = [(rhs_hbm.at[c], rhs.at[c]) for c in range(3)]
    pairs += [(zf_hbm, zf), (visc_hbm, visc_ref), (reac_hbm, reac_ref), (row_hbm, row), (lam_hbm, lam), (into_hbm, into), (outof_hbm, outof), (zb_hbm, zb)]
    for k, (src, dst) in enumerate(pairs):
        loads.append(pltpu.make_async_copy(src, dst, load_sem.at[k]))
        loads[-1].start()

    def pieces(rnd, c, d):
        dx, dy, dz = d
        full = 0 if rnd == 0 else 1
        if dz == 0 and dy == 0:
            return face.at[rnd, c, pl.ds(X_LAST if dx > 0 else X_FIRST, 32), :], rx.at[rnd, int(dx > 0), c]
        if dz == 0 and dx == 0:
            return face.at[rnd, c, pl.ds(Y_LAST if dy > 0 else Y_FIRST, 16), :], ry.at[rnd, int(dy > 0), c]
        if dz == 0:
            k = 2 * int(dx > 0) + int(dy > 0)
            return corner.at[full, k, c], rc.at[full, k, c]
        s = int(dz > 0)
        if dx == 0 and dy == 0:
            return zsend.at[rnd, s, c], rz.at[rnd, s, c]
        return zedge.at[full, s, c], re.at[full, s, slot(d), c]

    def slot(d):
        return 3 * (d[0] + 1) + d[1] + 1

    copies = {}
    for rnd in range(3):
        for c in range(3):
            for d in DIRS if rnd != 1 else FACES:
                k = len(copies)
                src, dst = pieces(rnd, c, d)
                copies[rnd, c, d] = pltpu.make_async_remote_copy(
                    src_ref=src, dst_ref=dst, send_sem=send_sem.at[k], recv_sem=recv_sem.at[k],
                    device_id=peer(d), device_id_type=MESH,
                )

    def send(rnd, c, ask):
        for (r, cc, d), copy in copies.items():
            if r == rnd and cc == c and ask(d):
                pl.when(exists(d))(copy.start)

    def arrive(rnd, c, ask=lambda d: True):
        for (r, cc, d), copy in copies.items():
            if r == rnd and cc == c and ask(d):
                pl.when(exists(minus(d)))(copy.wait_recv)

    flat = lambda d: d[2] == 0
    deep = lambda d: d[2] != 0

    for d in DIRS:
        @pl.when(jnp.logical_not(exists(minus(d))))
        def _(d=d):
            for rnd in range(3):
                if rnd != 1 or d in FACES:
                    for c in range(3):
                        dst = pieces(rnd, c, d)[1]
                        dst[...] = jnp.zeros(dst.shape, jnp.float32)

    zsend[...] = jnp.zeros(zsend.shape, jnp.float32)
    for k in range(4):
        ring[k, 32:40] = jnp.zeros((8, 128), jnp.float32)
        ring_end[k, 32:40] = jnp.zeros((8, 128), jnp.float32)

    lane = lax.broadcasted_iota(jnp.int32, (1, 128), 1)

    def by_element(ref, f, edge):
        v = jnp.zeros((1, 128), jnp.float32)
        for h in range(8):
            at = (lane >= edge * h) & (lane < edge * h + edge)
            v = jnp.where(at, ref[f, h], v)
        return v

    def fill_face(rnd, c, src):
        for k, y in enumerate((0, 15, 16, 31)):
            face[rnd, c, 16 * k : 16 * k + 8, :] = src[c, pl.ds(y, 8, stride=32), :]
            for x in range(8):
                at = 32 * (15 - x) + y
                face[rnd, c, 16 * k + 8 + x : 16 * k + 9 + x, :] = src[c, at : at + 1, :]
        face[rnd, c, X_FIRST : X_FIRST + 32, :] = src[c, 0:32]
        face[rnd, c, X_LAST : X_LAST + 32, :] = src[c, 480:512]

    def fill_corner(full, rnd, c):
        for k, at in enumerate((X_FIRST, X_FIRST + 31, X_LAST, X_LAST + 31)):
            corner[full, k, c] = face[rnd, c, at : at + 1, :]

    def z_forward(x):
        hi, lo = halves(x)
        return dot(jnp.concatenate([hi, lo, hi], axis=1), zf[...])

    def face_ends(rnd, c):
        hi, lo = halves(face[rnd, c])
        return dot(jnp.concatenate([hi, lo], axis=1), zf[:256, 128:])

    def gather_ends(ends, edge):
        total = ends[0]
        for k in range(1, 4):
            total = total + pltpu.roll(ends[k], k, 1)
        total = jnp.where(lane < HIGH + 4, total, pltpu.roll(edge, 16, 1))
        t = jnp.transpose(total)
        return t[LOW : LOW + 4], t[HIGH : HIGH + 4], t[LOW + 16 : LOW + 17], t[HIGH + 16 : HIGH + 17]

    def put_ends(rnd, c, low, high, edge_low, edge_high):
        for s, (planes, edge) in enumerate(((low, edge_low), (high, edge_high))):
            zsend[rnd, s, c, 0:4] = planes
            zsend[rnd, s, c, 4:5] = edge
            if rnd != 1:
                zedge[0 if rnd == 0 else 1, s, c] = edge

    def main_part(c, src):
        parts = []
        for f in range(2):
            near = [src[c, 32 * x + 16 * f : 32 * x + 16 * f + 16] for x in range(8)]
            far = [src[c, 32 * (15 - x) + 16 * f : 32 * (15 - x) + 16 * f + 16] for x in range(8)]
            parts += [n + m for n, m in zip(near, far)] + [n - m for n, m in zip(near, far)]
        m = z_forward(jnp.concatenate(parts, axis=0))
        ends = []
        for k in range(4):
            hi, lo = halves(m[128 * k : 128 * k + 128, :128])
            part_hi[c, k] = hi
            part_lo[c, k] = lo
            end = m[128 * k : 128 * k + 128, 128:]
            part_end[c, k] = end
            ends.append(end)
        return ends

    def ring_part(c, rnd, full):
        xm, xp = rx[rnd, 1, c], rx[rnd, 0, c]
        sums = (xm + xp, xm - xp)
        for p in range(2):
            fold = (lambda a, b: a + b) if p == 0 else (lambda a, b: a - b)
            ring[p, 0:16] = sums[p][0:16]
            ring[2 + p, 0:16] = sums[p][16:32]
            ym, yp = ry[rnd, 1, c], ry[rnd, 0, c]
            mid = face[rnd, c, Y_MID : Y_MID + 32]
            ring[p, 16:24] = fold(ym[0:8], ym[8:16])
            ring[p, 24:32] = fold(mid[16:24], mid[24:32])
            ring[2 + p, 16:24] = fold(mid[0:8], mid[8:16])
            ring[2 + p, 24:32] = fold(yp[0:8], yp[8:16])
            ring[p, 32:33] = fold(rc[full, 3, c], rc[full, 1, c])
            ring[p, 33:34] = sums[p][16:17]
            ring[2 + p, 32:33] = sums[p][15:16]
            ring[2 + p, 33:34] = fold(rc[full, 2, c], rc[full, 0, c])
        return z_forward(ring[...].reshape(4 * RING, 128))

    def ring_planes(c, full, rnd):
        rows = []
        for s in (1, 0):
            got = lambda dx, dy: re[full, s, slot((dx, dy)), c]
            own = rz[rnd, s, c, 4:5]
            t = jnp.where((lane >= 48) & (lane < 64), got(0, 1), own)
            t = jnp.where((lane >= 64) & (lane < 95), got(-1, 0), t)
            t = jnp.where(lane == 95, got(-1, 1), t)
            t = jnp.where((lane >= 96) & (lane < 127), got(1, 0), t)
            t = jnp.where(lane == 127, got(1, 1), t)
            rows += [t, t]
            t = jnp.where(lane < 16, got(0, -1), own)
            t = jnp.where(lane == 64, got(-1, -1), t)
            t = jnp.where((lane > 64) & (lane < 96), got(-1, 0), t)
            t = jnp.where(lane == 96, got(1, -1), t)
            t = jnp.where(lane > 96, got(1, 0), t)
            rows += [t, t]
        t = jnp.concatenate([jnp.zeros((56, 128), jnp.float32)] + rows + [jnp.zeros((64, 128), jnp.float32)], axis=0)
        t = jnp.transpose(t)
        for p in range(2):
            fold = (lambda a, b: a + b) if p == 0 else (lambda a, b: a - b)
            ends = fold(t[96:128], t[64:96])
            ring_end[p, 0:16] = ends[0:16]
            ring_end[2 + p, 0:16] = ends[16:32]
            ring_end[p, 16:24] = fold(t[48:56], t[56:64])
            ring_end[p, 24:32] = fold(t[32:40], t[40:48])
            ring_end[2 + p, 16:24] = fold(t[16:24], t[24:32])
            ring_end[2 + p, 24:32] = fold(t[0:8], t[8:16])
            ring_end[p, 32:33] = ends[31:32]
            ring_end[p, 33:34] = ends[16:17]
            ring_end[2 + p, 32:33] = ends[15:16]
            ring_end[2 + p, 33:34] = ends[0:1]

    def solve(c, rnd, full, inner):
        around = ring_part(c, rnd, full)
        ring_planes(c, full, rnd)
        blank = jnp.zeros((56, 128), jnp.float32)
        planes = [blank, rz[rnd, 1, c, 0:4], rz[rnd, 0, c, 0:4]]
        planes += [blank, jnp.zeros((8, 128), jnp.float32)] if inner is None else [inner, blank]
        planes = jnp.transpose(jnp.concatenate(planes, axis=0))
        outs = []
        for k in range(4):
            f, p = k // 2, k % 2
            eh, el = halves(jnp.where(lane < 48, part_end[c, k], planes))
            hi = jnp.concatenate([part_hi[c, k], eh], axis=1)
            lo = jnp.concatenate([part_lo[c, k], el], axis=1)
            r = around[RING * k : RING * k + RING]
            r = jnp.concatenate([r[:, :128], jnp.where(lane < 48, r[:, 128:], ring_end[k])], axis=1)
            rh, rl = wide_halves(r)
            r = jnp.concatenate([rh, rl, rh, jnp.zeros((8, 256), jnp.float32)], axis=0).astype(jnp.bfloat16)
            m = dot(into[p], jnp.concatenate([hi, lo, hi, r], axis=0))[:HALF]
            t = m + m[:, 128 + LOW + k : 129 + LOW + k] * row[0:1]
            t = t + m[:, 128 + HIGH + k : 129 + HIGH + k] * row[1:2]
            if inner is not None:
                t = t + m[:, 136 + LOW + k : 137 + LOW + k] * row[2:3]
                t = t + m[:, 136 + HIGH + k : 137 + HIGH + k] * row[3:4]
            th, tl = wide_halves(t * inv[k])
            data = jnp.concatenate([th, tl, th, jnp.zeros((8, 256), jnp.float32)], axis=0).astype(jnp.bfloat16)
            u = dot(outof[p], data)
            hi, lo = halves(u[:, :128])
            eh, el = wide_halves(u[:, 128:])
            end = jnp.where((lane >= 16) & (lane < 32), el, eh).astype(jnp.bfloat16)
            outs.append(jnp.concatenate([hi, lo, hi, end], axis=1))
        return jnp.concatenate(outs, axis=0)

    def unfold(x, put):
        for f in range(2):
            for i in range(8):
                s = x[256 * f + 16 * i : 256 * f + 16 * i + 16, :128]
                d = x[256 * f + 128 + 16 * i : 256 * f + 128 + 16 * i + 16, :128]
                put(32 * i + 16 * f, s + d)
                put(32 * (15 - i) + 16 * f, s - d)

    for c in range(3):
        loads[c].wait()
        fill_face(0, c, rhs)
        fill_corner(0, 0, c)
    loads[3].wait()
    for c in range(3):
        ends = main_part(c, rhs)
        put_ends(0, c, *gather_ends(ends, face_ends(0, c)))
    pl.semaphore_wait(barrier, count)
    for c in range(3):
        send(0, c, lambda d: True)
    for k in range(4, 11):
        loads[k].wait()

    for f in range(2):
        for t in range(2):
            part = slice(128 * t, 128 * t + 128)
            if t == 0:
                v, r = by_element(visc_ref, f, SPAN), by_element(reac_ref, f, SPAN)
                v = jnp.where(lane >= 7 * SPAN, visc_ref[f, 7], v)
                r = jnp.where(lane >= 7 * SPAN, reac_ref[f, 7], r)
            else:
                v, r = jnp.full((1, 128), visc_ref[f, 7]), jnp.full((1, 128), reac_ref[f, 7])
            for p in range(2):
                inv[2 * f + p, :, part] = 1.0 / (v * (lam[p] + row[4:5, part]) + r)
        v, r = by_element(visc_ref, f, EDGE), by_element(reac_ref, f, EDGE)
        visc_plane[16 * f : 16 * f + 16] = jnp.broadcast_to(v, (16, 128))
        coef_plane[16 * f : 16 * f + 16] = jnp.broadcast_to(r + 6.0 * v, (16, 128))

    part_row = lax.broadcasted_iota(jnp.int32, (4, 128), 0)
    upper = ((lane >= 32) & (lane < 64)) | ((lane >= 80) & (lane < 96)) | (lane >= 112)
    plane_visc = [jnp.where(part_row < 2, visc_ref[0, h], visc_ref[1, h]) for h in (0, 7)]
    edge_visc = [jnp.where(upper, visc_ref[1, h], visc_ref[0, h]) for h in (0, 7)]

    for c in range(3):
        arrive(0, c)
        lhs = solve(c, 0, 0, None)
        x = dot(lhs, zb[...])

        def put_first(at, v, c=c):
            first[c, at : at + 16] = v

        unfold(x, put_first)
        fill_face(1, c, first)
        send(1, c, flat)
        ends = [x[128 * k : 128 * k + 128, 128:] for k in range(4)]
        put_ends(1, c, *gather_ends(ends, face_ends(1, c)))
        send(1, c, deep)

    y_index = lax.broadcasted_iota(jnp.int32, (32, 128), 0)
    inner = []
    for c in range(3):
        arrive(1, c)
        for x in range(16):
            v = first[c, 32 * x : 32 * x + 32]
            beside = rx[1, 1, c] if x == 0 else first[c, 32 * x - 32 : 32 * x]
            beside = beside + (rx[1, 0, c] if x == 15 else first[c, 32 * x + 32 : 32 * x + 64])
            at = x if x < 8 else 23 - x
            ylo, yhi = ry[1, 1, c, at : at + 1], ry[1, 0, c, at : at + 1]
            beside = beside + jnp.where(y_index == 0, ylo, pltpu.roll(v, 1, 0))
            beside = beside + jnp.where(y_index == 31, yhi, pltpu.roll(v, 31, 0))
            beside = beside + jnp.where(lane == 0, 0.0, pltpu.roll(v, 1, 1))
            beside = beside + jnp.where(lane == 127, 0.0, pltpu.roll(v, 127, 1))
            resid[c, 32 * x : 32 * x + 32] = (
                rhs[c, 32 * x : 32 * x + 32] - coef_plane[...] * v + visc_plane[...] * beside
            )
        fill_face(2, c, resid)
        planes = [plane_visc[s] * rz[1, 1 - s, c, 0:4] for s in range(2)]
        edge = [edge_visc[s] * rz[1, 1 - s, c, 4:5] for s in range(2)]
        inner.append(jnp.concatenate(planes, axis=0))
        face_low_high = face_ends(2, c)
        add = jnp.transpose(
            jnp.concatenate([edge[0], jnp.zeros((126, 128), jnp.float32), edge[1]], axis=0)
        )
        face[2, c] = face[2, c] + add
        fill_corner(1, 2, c)
        send(2, c, flat)
        ends = main_part(c, resid)
        low, high, edge_low, edge_high = gather_ends(ends, face_low_high)
        put_ends(2, c, low + planes[0], high + planes[1], edge_low + edge[0], edge_high + edge[1])
        send(2, c, deep)

    for c in range(3):
        arrive(2, c)
        lhs = solve(c, 2, 1, inner[c])
        x = dot(lhs, zb[:, :128])

        def put_last(at, v, c=c):
            out_ref[c, at : at + 16] = first[c, at : at + 16] + v

        unfold(x, put_last)

    for (rnd, c, d), copy in copies.items():
        pl.when(exists(d))(copy.wait_send)


def shards(sizes, rhs, viscous, reaction):
    f32, bf16 = jnp.float32, jnp.bfloat16
    consts = constants()
    any_space = pl.BlockSpec(memory_space=pl.ANY)
    vmem = pl.BlockSpec(memory_space=pltpu.VMEM)
    copies = 3 * (2 * len(DIRS) + len(FACES))
    scratch = [
        pltpu.VMEM((3, 512, 128), f32),
        pltpu.VMEM((3, 512, 128), f32),
        pltpu.VMEM((3, 512, 128), f32),
        pltpu.VMEM((3, 3, 128, 128), f32),
        pltpu.VMEM((2, 4, 3, 1, 128), f32),
        pltpu.VMEM((3, 2, 3, 8, 128), f32),
        pltpu.VMEM((2, 2, 3, 1, 128), f32),
        pltpu.VMEM((3, 2, 3, 32, 128), f32),
        pltpu.VMEM((3, 2, 3, 16, 128), f32),
        pltpu.VMEM((2, 4, 3, 1, 128), f32),
        pltpu.VMEM((3, 2, 3, 8, 128), f32),
        pltpu.VMEM((2, 2, 9, 3, 1, 128), f32),
        pltpu.VMEM((3, 4, 128, 128), bf16),
        pltpu.VMEM((3, 4, 128, 128), bf16),
        pltpu.VMEM((3, 4, 128, 128), f32),
        pltpu.VMEM((4, RING, 128), f32),
        pltpu.VMEM((4, RING, 128), f32),
        pltpu.VMEM((4, HALF, 256), f32),
        pltpu.VMEM((32, 128), f32),
        pltpu.VMEM((32, 128), f32),
    ]
    scratch += [pltpu.VMEM(t.shape, t.dtype) for t in consts]
    scratch += [
        pltpu.SMEM((2, 8), f32),
        pltpu.SMEM((2, 8), f32),
        pltpu.SemaphoreType.DMA((11,)),
        pltpu.SemaphoreType.DMA((copies,)),
        pltpu.SemaphoreType.DMA((copies,)),
    ]
    operands = (rhs.reshape(3, 512, 128), viscous.reshape(2, 8), reaction.reshape(2, 8), *consts)
    out = pl.pallas_call(
        functools.partial(kernel, sizes),
        out_shape=jax.ShapeDtypeStruct((3, 512, 128), f32),
        in_specs=[any_space] * len(operands),
        out_specs=vmem,
        scratch_shapes=scratch,
        compiler_params=pltpu.CompilerParams(
            collective_id=0, has_side_effects=True, vmem_limit_bytes=40 * 2**20
        ),
    )(*[pltpu.with_memory_space_constraint(jnp.asarray(a), pltpu.HBM) for a in operands])
    return out.reshape(rhs.shape)


def solution(mesh):
    sizes = tuple(mesh.shape[a] for a in ("gx", "gy", "gz"))
    placed = (P(None, "gx", "gy", "gz"), P("gx", "gy", "gz"), P("gx", "gy", "gz"))
    return jax.shard_map(
        functools.partial(shards, sizes),
        mesh=mesh,
        in_specs=placed,
        out_specs=P(None, "gx", "gy", "gz"),
        check_vma=False,
    )
```

profile of v0, /device:TPU:1, one launch (start us, length us, event | category | flops | bytes accessed | tf_op | source)
XLA Modules:
  0.0 38.5 jit_solution(2688010050753167455)
XLA Ops:
  0.0 37.6 %shard_map.91 = f32[3,512,128]{2,1,0:T(8,128)S(1)} custom-call(f32[3,512,128]{2,1,0:T(8,128)} %bitcast.5, f32[2,8]{1,0:T(2,128)} %bitcast.6, f32[2,8]{1,0:T(2,128)} %bitcast.7, bf16[384,256]{1,0:T(8,128)(2,1)} %constant.12.clone.zf_hbm, bf16[2,176,512]{2,1,0:T(8,128)(2,1)} %constant.13.clone.into_hbm, bf16[2,128,512]{2,1,0:T(8,128)(2,1)} %constant.14.clone.outof_hbm, ...), custom_call_target="tpu_custom_call" | custom-call | tf_op jit(solution)/shard_map/pallas_call | solution.py:496
  37.6 0.9 %copy.11 = f32[3,16,32,128]{3,2,1,0:T(8,128)} copy(f32[3,16,32,128]{3,2,1,0:T(8,128)S(1)} %bitcast.4) | data formatting | bytes 1572864
where the time goes:
time: 38.6 us; the launch traced here: 38.5 us
  Pallas kernels  37.6 us (97%)
  local copies, waits for them, and re-layouts  0.88 us (2%)
    pallas_call x1, Pallas kernels, shards(): pl.pallas_call(functools.partial(kernel, sizes), out_shape=jax.ShapeDtype...  37.6 us
    unnamed x1, local copies, waits for them, and re-layouts  0.88 us

commit v1 on v0

--- a/solution.py
+++ b/solution.py
@@ -327,9 +327,8 @@
         planes = [blank, rz[rnd, 1, c, 0:4], rz[rnd, 0, c, 0:4]]
         planes += [blank, jnp.zeros((8, 128), jnp.float32)] if inner is None else [inner, blank]
         planes = jnp.transpose(jnp.concatenate(planes, axis=0))
-        outs = []
+        ms = []
         for k in range(4):
-            f, p = k // 2, k % 2
             eh, el = halves(jnp.where(lane < 48, part_end[c, k], planes))
             hi = jnp.concatenate([part_hi[c, k], eh], axis=1)
             lo = jnp.concatenate([part_lo[c, k], el], axis=1)
@@ -337,7 +336,10 @@
             r = jnp.concatenate([r[:, :128], jnp.where(lane < 48, r[:, 128:], ring_end[k])], axis=1)
             rh, rl = wide_halves(r)
             r = jnp.concatenate([rh, rl, rh, jnp.zeros((8, 256), jnp.float32)], axis=0).astype(jnp.bfloat16)
-            m = dot(into[p], jnp.concatenate([hi, lo, hi, r], axis=0))[:HALF]
+            ms.append(dot(into[k % 2], jnp.concatenate([hi, lo, hi, r], axis=0))[:HALF])
+        us = []
+        for k in range(4):
+            m = ms[k]
             t = m + m[:, 128 + LOW + k : 129 + LOW + k] * row[0:1]
             t = t + m[:, 128 + HIGH + k : 129 + HIGH + k] * row[1:2]
             if inner is not None:
@@ -345,7 +347,9 @@
                 t = t + m[:, 136 + HIGH + k : 137 + HIGH + k] * row[3:4]
             th, tl = wide_halves(t * inv[k])
             data = jnp.concatenate([th, tl, th, jnp.zeros((8, 256), jnp.float32)], axis=0).astype(jnp.bfloat16)
-            u = dot(outof[p], data)
+            us.append(dot(outof[k % 2], data))
+        outs = []
+        for u in us:
             hi, lo = halves(u[:, :128])
             eh, el = wide_halves(u[:, 128:])
             end = jnp.where((lane >= 16) & (lane < 32), el, eh).astype(jnp.bfloat16)

time: 38.6 us -> 35.2 us (0.912)
  Pallas kernels: 37.6 us -> 34.2 us
    pallas_call x1, Pallas kernels: 37.6 us -> 34.2 us  [shards(): pl.pallas_call(functools.partial(kernel, sizes), out_shape=jax.ShapeDtype...]
where the time goes in v1:
time: 35.2 us; the launch traced here: 35.1 us
  Pallas kernels  34.2 us (97%)
  local copies, waits for them, and re-layouts  0.88 us (2%)
    pallas_call x1, Pallas kernels, shards(): pl.pallas_call(functools.partial(kernel, sizes), out_shape=jax.ShapeDtype...  34.2 us
    unnamed x1, local copies, waits for them, and re-layouts  0.88 us

profile of v1, /device:TPU:1, one launch (start us, length us, event | category | flops | bytes accessed | tf_op | source)
XLA Modules:
  0.0 35.1 jit_solution(6109482311925803305)
XLA Ops:
  0.0 34.2 %shard_map.91 = f32[3,512,128]{2,1,0:T(8,128)S(1)} custom-call(f32[3,512,128]{2,1,0:T(8,128)} %bitcast.5, f32[2,8]{1,0:T(2,128)} %bitcast.6, f32[2,8]{1,0:T(2,128)} %bitcast.7, bf16[384,256]{1,0:T(8,128)(2,1)} %constant.12.clone.zf_hbm, bf16[2,176,512]{2,1,0:T(8,128)(2,1)} %constant.13.clone.into_hbm, bf16[2,128,512]{2,1,0:T(8,128)(2,1)} %constant.14.clone.outof_hbm, ...), custom_call_target="tpu_custom_call" | custom-call | tf_op jit(solution)/shard_map/pallas_call | solution.py:500
  34.2 0.9 %copy.11 = f32[3,16,32,128]{3,2,1,0:T(8,128)} copy(f32[3,16,32,128]{3,2,1,0:T(8,128)S(1)} %bitcast.4) | data formatting | bytes 1572864

commit v2 on v1

--- a/solution.py
+++ b/solution.py
@@ -12,7 +12,8 @@
 SPAN = EDGE + 2
 HALF = 168
 RING = 40
-LOW, HIGH = 56, 60
+TAIL = 3 * SPAN
+LOW, HIGH = 64, 68
 MESH = pl.DeviceIdType.MESH
 NN = (((1,), (0,)), ((), ()))
 DIRS = [
@@ -36,8 +37,7 @@
     i = np.arange(SPAN)
     basis = np.sqrt(2.0 / (SPAN + 1)) * np.sin(np.pi * np.outer(i + 1, i + 1) / (SPAN + 1))
     lam = 2.0 - 2.0 * np.cos(np.pi * (i + 1) / (SPAN + 1))
-    q = np.arange(144)
-    lanes = np.concatenate([np.arange(128), np.tile(np.arange(128, 144), 3)])
+    lanes = np.concatenate([np.arange(126), [-1, -1], np.tile(np.arange(126, 144), 3)])
     forward = np.zeros((128, 256))
     back = np.zeros((144, 128))
     for h in range(8):
@@ -45,7 +45,7 @@
             w = z - EDGE * h + 1
             if 0 <= w < SPAN:
                 for n, k in enumerate(lanes):
-                    if k // SPAN == h:
+                    if k >= 0 and k // SPAN == h:
                         forward[z, n] = basis[w, k % SPAN]
             if 1 <= w <= EDGE:
                 back[h * SPAN : (h + 1) * SPAN, z] = basis[w]
@@ -58,8 +58,9 @@
     fh, fl = table_halves(forward)
     bh, bl = table_halves(wide)
     z_forward = np.concatenate([fh, fh, fl], axis=0)
+    pad = lambda n: np.zeros((n, 256), bh.dtype)
     z_back = np.concatenate(
-        [bh[:128], bh[:128], bl[:128], bh[128:], bh[128:], bl[128:], np.zeros((80, 256), bh.dtype)], axis=0
+        [bh[:126], pad(2), bh[:126], pad(2), bl[:126], pad(2), bh[126:], bh[126:], bl[126:], pad(74)], axis=0
     )
     into, out_of, lam_xy = [], [], []
     for parity in range(2):
@@ -80,13 +81,20 @@
         mh, ml = table_halves(main)
         rh, rl = table_halves(ring)
         into.append(np.concatenate([mh, mh, ml, rh, rh, rl, np.zeros((176, 8), mh.dtype)], axis=1))
-        th, tl = mh[:HALF].T, ml[:HALF].T
-        out_of.append(np.concatenate([th, th, tl, np.zeros((128, 8), mh.dtype)], axis=1))
         col = np.zeros((HALF, 1))
         col[:162, 0] = lam[a] + lam[b]
+        th, tl = mh[:HALF].T, ml[:HALF].T
+        a, b = slice(0, 128), slice(128, HALF)
+        out_of.append(
+            np.concatenate(
+                [th[:, a], th[:, a], tl[:, a], th[:, b], th[:, b], tl[:, b], np.zeros((128, 8), mh.dtype)], axis=1
+            )
+        )
         lam_xy.append(np.repeat(col, 128, 1))
     rows = np.zeros((8, 256))
     for n, k in enumerate(lanes):
+        if k < 0:
+            continue
         if k < SPAN:
             rows[0, n], rows[2, n] = basis[0, k], basis[1, k]
         if k >= 7 * SPAN:
@@ -114,8 +122,8 @@
     sizes, rhs_hbm, visc_hbm, reac_hbm, zf_hbm, into_hbm, outof_hbm, zb_hbm, row_hbm, lam_hbm,
     out_ref,
     rhs, first, resid, face, corner, zsend, zedge, rx, ry, rc, rz, re,
-    part_hi, part_lo, part_end, ring, ring_end, inv, visc_plane, coef_plane,
-    zf, into, outof, zb, row, lam, visc_ref, reac_ref, load_sem, send_sem, recv_sem,
+    part_hi, part_lo, end_hi, end_lo, ring, ring_end, inv, visc_plane, coef_plane,
+    zf, into, outof, zb, row, lam, visc_ref, reac_ref, load_sem, send_sem, recv_sem, token,
 ):
     me = tuple(lax.axis_index(a) for a in ("gx", "gy", "gz"))
 
@@ -133,22 +141,28 @@
     def minus(d):
         return tuple(-s for s in d)
 
+    def greet(sem, dirs):
+        count = jnp.int32(0)
+        for d in dirs:
+            ok = exists(d)
+            count = count + ok.astype(jnp.int32)
+
+            @pl.when(ok)
+            def _(d=d):
+                pl.semaphore_signal(sem, inc=1, device_id=peer(d), device_id_type=MESH)
+
+        return count
+
     barrier = pltpu.get_barrier_semaphore()
-    count = jnp.int32(0)
-    for d in DIRS:
-        ok = exists(d)
-        count = count + ok.astype(jnp.int32)
-
-        @pl.when(ok)
-        def _(d=d):
-            pl.semaphore_signal(barrier, inc=1, device_id=peer(d), device_id_type=MESH)
+    count = greet(barrier, FACES)
 
     loads = []
     pairs = [(rhs_hbm.at[c], rhs.at[c]) for c in range(3)]
     pairs += [(zf_hbm, zf), (visc_hbm, visc_ref), (reac_hbm, reac_ref), (row_hbm, row), (lam_hbm, lam), (into_hbm, into), (outof_hbm, outof), (zb_hbm, zb)]
     for k, (src, dst) in enumerate(pairs):
         loads.append(pltpu.make_async_copy(src, dst, load_sem.at[k]))
-        loads[-1].start()
+    for load in loads[:4]:
+        load.start()
 
     def pieces(rnd, c, d):
         dx, dy, dz = d
@@ -159,10 +173,14 @@
             return face.at[rnd, c, pl.ds(Y_LAST if dy > 0 else Y_FIRST, 16), :], ry.at[rnd, int(dy > 0), c]
         if dz == 0:
             k = 2 * int(dx > 0) + int(dy > 0)
+            if rnd == 0:
+                return corner.at[0, k], rc.at[0, k]
             return corner.at[full, k, c], rc.at[full, k, c]
         s = int(dz > 0)
         if dx == 0 and dy == 0:
             return zsend.at[rnd, s, c], rz.at[rnd, s, c]
+        if rnd == 0:
+            return zedge.at[0, s], re.at[0, s, slot(d)]
         return zedge.at[full, s, c], re.at[full, s, slot(d), c]
 
     def slot(d):
@@ -171,7 +189,7 @@
     copies = {}
     for rnd in range(3):
         for c in range(3):
-            for d in DIRS if rnd != 1 else FACES:
+            for d in DIRS if rnd == 2 or (rnd, c) == (0, 0) else FACES:
                 k = len(copies)
                 src, dst = pieces(rnd, c, d)
                 copies[rnd, c, d] = pltpu.make_async_remote_copy(
@@ -189,22 +207,13 @@
             if r == rnd and cc == c and ask(d):
                 pl.when(exists(minus(d)))(copy.wait_recv)
 
+    def drain(rnd, which):
+        for (r, c, d), copy in copies.items():
+            if r == rnd and c in which:
+                pl.when(exists(d))(copy.wait_send)
+
     flat = lambda d: d[2] == 0
     deep = lambda d: d[2] != 0
-
-    for d in DIRS:
-        @pl.when(jnp.logical_not(exists(minus(d))))
-        def _(d=d):
-            for rnd in range(3):
-                if rnd != 1 or d in FACES:
-                    for c in range(3):
-                        dst = pieces(rnd, c, d)[1]
-                        dst[...] = jnp.zeros(dst.shape, jnp.float32)
-
-    zsend[...] = jnp.zeros(zsend.shape, jnp.float32)
-    for k in range(4):
-        ring[k, 32:40] = jnp.zeros((8, 128), jnp.float32)
-        ring_end[k, 32:40] = jnp.zeros((8, 128), jnp.float32)
 
     lane = lax.broadcasted_iota(jnp.int32, (1, 128), 1)
 
@@ -264,7 +273,9 @@
             part_hi[c, k] = hi
             part_lo[c, k] = lo
             end = m[128 * k : 128 * k + 128, 128:]
-            part_end[c, k] = end
+            hi, lo = halves(jnp.where(lane < TAIL, end, 0.0))
+            end_hi[c, k] = hi
+            end_lo[c, k] = lo
             ends.append(end)
         return ends
 
@@ -304,7 +315,7 @@
             t = jnp.where(lane == 96, got(1, -1), t)
             t = jnp.where(lane > 96, got(1, 0), t)
             rows += [t, t]
-        t = jnp.concatenate([jnp.zeros((56, 128), jnp.float32)] + rows + [jnp.zeros((64, 128), jnp.float32)], axis=0)
+        t = jnp.concatenate([jnp.zeros((LOW, 128), jnp.float32)] + rows + [jnp.zeros((120 - LOW, 128), jnp.float32)], axis=0)
         t = jnp.transpose(t)
         for p in range(2):
             fold = (lambda a, b: a + b) if p == 0 else (lambda a, b: a - b)
@@ -323,36 +334,39 @@
     def solve(c, rnd, full, inner):
         around = ring_part(c, rnd, full)
         ring_planes(c, full, rnd)
-        blank = jnp.zeros((56, 128), jnp.float32)
-        planes = [blank, rz[rnd, 1, c, 0:4], rz[rnd, 0, c, 0:4]]
-        planes += [blank, jnp.zeros((8, 128), jnp.float32)] if inner is None else [inner, blank]
-        planes = jnp.transpose(jnp.concatenate(planes, axis=0))
+        blank = lambda n: jnp.zeros((n, 128), jnp.float32)
+        planes = [blank(LOW), rz[rnd, 1, c, 0:4], rz[rnd, 0, c, 0:4]]
+        planes += [blank(8) if inner is None else inner, blank(112 - LOW)]
+        plane_hi, plane_lo = halves(jnp.transpose(jnp.concatenate(planes, axis=0)))
         ms = []
         for k in range(4):
-            eh, el = halves(jnp.where(lane < 48, part_end[c, k], planes))
-            hi = jnp.concatenate([part_hi[c, k], eh], axis=1)
-            lo = jnp.concatenate([part_lo[c, k], el], axis=1)
+            hi = jnp.concatenate([part_hi[c, k], end_hi[c, k] + plane_hi], axis=1)
+            lo = jnp.concatenate([part_lo[c, k], end_lo[c, k] + plane_lo], axis=1)
             r = around[RING * k : RING * k + RING]
-            r = jnp.concatenate([r[:, :128], jnp.where(lane < 48, r[:, 128:], ring_end[k])], axis=1)
+            r = jnp.concatenate([r[:, :128], jnp.where(lane < TAIL, r[:, 128:], ring_end[k])], axis=1)
             rh, rl = wide_halves(r)
             r = jnp.concatenate([rh, rl, rh, jnp.zeros((8, 256), jnp.float32)], axis=0).astype(jnp.bfloat16)
             ms.append(dot(into[k % 2], jnp.concatenate([hi, lo, hi, r], axis=0))[:HALF])
         us = []
         for k in range(4):
             m = ms[k]
-            t = m + m[:, 128 + LOW + k : 129 + LOW + k] * row[0:1]
-            t = t + m[:, 128 + HIGH + k : 129 + HIGH + k] * row[1:2]
+            column = lambda n: m[:, 128 + n + k : 129 + n + k]
+            low = m[:, :128] + column(LOW) * row[0:1, :128]
+            high = m[:, 128:] + column(HIGH) * row[1:2, 128:]
             if inner is not None:
-                t = t + m[:, 136 + LOW + k : 137 + LOW + k] * row[2:3]
-                t = t + m[:, 136 + HIGH + k : 137 + HIGH + k] * row[3:4]
-            th, tl = wide_halves(t * inv[k])
-            data = jnp.concatenate([th, tl, th, jnp.zeros((8, 256), jnp.float32)], axis=0).astype(jnp.bfloat16)
+                low = low + column(LOW + 8) * row[2:3, :128]
+                high = high + column(HIGH + 8) * row[3:4, 128:]
+            t = jnp.concatenate([low, high], axis=1) * inv[k]
+            hi, lo = halves(t[:128])
+            th, tl = wide_halves(t[128:])
+            t = jnp.concatenate([th, tl, th, jnp.zeros((8, 256), jnp.float32)], axis=0).astype(jnp.bfloat16)
+            data = jnp.concatenate([hi, lo, hi, t], axis=0)
             us.append(dot(outof[k % 2], data))
         outs = []
         for u in us:
             hi, lo = halves(u[:, :128])
             eh, el = wide_halves(u[:, 128:])
-            end = jnp.where((lane >= 16) & (lane < 32), el, eh).astype(jnp.bfloat16)
+            end = jnp.where((lane >= SPAN) & (lane < 2 * SPAN), el, eh).astype(jnp.bfloat16)
             outs.append(jnp.concatenate([hi, lo, hi, end], axis=1))
         return jnp.concatenate(outs, axis=0)
 
@@ -368,13 +382,42 @@
         loads[c].wait()
         fill_face(0, c, rhs)
         fill_corner(0, 0, c)
+    pl.semaphore_wait(barrier, count)
+    for c in range(3):
+        send(0, c, lambda d: d in FACES and d[1] != 0)
+    count = greet(token.at[0], [d for d in FACES if d[1] == 0])
+    for c in range(3):
+        send(0, c, lambda d: d in FACES and d[0] != 0)
+    for load in loads[4:]:
+        load.start()
+    zsend[...] = jnp.zeros(zsend.shape, jnp.float32)
+    for k in range(4):
+        ring[k, 32:40] = jnp.zeros((8, 128), jnp.float32)
+        ring_end[k, 32:40] = jnp.zeros((8, 128), jnp.float32)
+
     loads[3].wait()
     for c in range(3):
         ends = main_part(c, rhs)
         put_ends(0, c, *gather_ends(ends, face_ends(0, c)))
-    pl.semaphore_wait(barrier, count)
-    for c in range(3):
-        send(0, c, lambda d: True)
+    pl.semaphore_wait(token.at[0], count)
+    count = greet(token.at[1], [d for d in FACES if d[2] != 0])
+    for c in range(3):
+        send(0, c, lambda d: sum(map(abs, d)) == 2 and d[1] != 0)
+    for c in range(3):
+        send(0, c, lambda d: d[1] == 0 and d[2] != 0)
+    pl.semaphore_wait(token.at[1], count)
+    for c in range(3):
+        send(0, c, lambda d: sum(map(abs, d)) == 3)
+
+    for d in DIRS:
+        @pl.when(jnp.logical_not(exists(minus(d))))
+        def _(d=d):
+            for rnd in range(3):
+                for c in range(3):
+                    if d in FACES or rnd == 2 or (rnd, c) == (0, 0):
+                        dst = pieces(rnd, c, d)[1]
+                        dst[...] = jnp.zeros(dst.shape, jnp.float32)
+
     for k in range(4, 11):
         loads[k].wait()
 
@@ -446,7 +489,11 @@
         put_ends(2, c, low + planes[0], high + planes[1], edge_low + edge[0], edge_high + edge[1])
         send(2, c, deep)
 
-    for c in range(3):
+    drain(0, (0, 1, 2))
+    drain(1, (0, 1, 2))
+    for c in range(3):
+        if c:
+            drain(2, (c - 1,))
         arrive(2, c)
         lhs = solve(c, 2, 1, inner[c])
         x = dot(lhs, zb[:, :128])
@@ -456,8 +503,7 @@
 
         unfold(x, put_last)
 
-    for (rnd, c, d), copy in copies.items():
-        pl.when(exists(d))(copy.wait_send)
+    drain(2, (2,))
 
 
 def shards(sizes, rhs, viscous, reaction):
@@ -481,7 +527,8 @@
         pltpu.VMEM((2, 2, 9, 3, 1, 128), f32),
         pltpu.VMEM((3, 4, 128, 128), bf16),
         pltpu.VMEM((3, 4, 128, 128), bf16),
-        pltpu.VMEM((3, 4, 128, 128), f32),
+        pltpu.VMEM((3, 4, 128, 128), bf16),
+        pltpu.VMEM((3, 4, 128, 128), bf16),
         pltpu.VMEM((4, RING, 128), f32),
         pltpu.VMEM((4, RING, 128), f32),
         pltpu.VMEM((4, HALF, 256), f32),
@@ -495,6 +542,7 @@
         pltpu.SemaphoreType.DMA((11,)),
         pltpu.SemaphoreType.DMA((copies,)),
         pltpu.SemaphoreType.DMA((copies,)),
+        pltpu.SemaphoreType.REGULAR((2,)),
     ]
     operands = (rhs.reshape(3, 512, 128), viscous.reshape(2, 8), reaction.reshape(2, 8), *consts)
     out = pl.pallas_call(

time: 35.2 us -> 34.8 us (0.989)
  Pallas kernels: 34.2 us -> 33.8 us
    pallas_call x1, Pallas kernels: 34.2 us -> 33.8 us  [shards(): pl.pallas_call(functools.partial(kernel, sizes), out_shape=jax.ShapeDtype...]
where the time goes in v2:
time: 34.8 us; the launch traced here: 34.7 us
  Pallas kernels  33.8 us (97%)
  local copies, waits for them, and re-layouts  0.88 us (3%)
    pallas_call x1, Pallas kernels, shards(): pl.pallas_call(functools.partial(kernel, sizes), out_shape=jax.ShapeDtype...  33.8 us
    unnamed x1, local copies, waits for them, and re-layouts  0.88 us

profile of v2, /device:TPU:1, one launch (start us, length us, event | category | flops | bytes accessed | tf_op | source)
XLA Modules:
  0.0 34.7 jit_solution(12138496648181927853)
XLA Ops:
  0.0 33.8 %shard_map.91 = f32[3,512,128]{2,1,0:T(8,128)S(1)} custom-call(f32[3,512,128]{2,1,0:T(8,128)} %bitcast.5, f32[2,8]{1,0:T(2,128)} %bitcast.6, f32[2,8]{1,0:T(2,128)} %bitcast.7, bf16[384,256]{1,0:T(8,128)(2,1)} %constant.12.clone.zf_hbm, bf16[2,176,512]{2,1,0:T(8,128)(2,1)} %constant.13.clone.into_hbm, bf16[2,128,512]{2,1,0:T(8,128)(2,1)} %constant.14.clone.outof_hbm, ...), custom_call_target="tpu_custom_call" | custom-call | tf_op jit(solution)/shard_map/pallas_call | solution.py:548
  33.8 0.9 %copy.11 = f32[3,16,32,128]{3,2,1,0:T(8,128)} copy(f32[3,16,32,128]{3,2,1,0:T(8,128)S(1)} %bitcast.4) | data formatting | bytes 1572864

commit v3 on v2

--- a/solution.py
+++ b/solution.py
@@ -198,7 +198,7 @@
                 )
 
     def send(rnd, c, ask):
-        for (r, cc, d), copy in copies.items():
+        for (r, cc, d), copy in sorted(copies.items(), key=lambda item: -abs(item[0][2][1])):
             if r == rnd and cc == c and ask(d):
                 pl.when(exists(d))(copy.start)
 

time: 34.8 us -> 34.7 us (level)
  no operation moved by 1% of the time
where the time goes in v3:
time: 34.7 us; the launch traced here: 34.6 us
  Pallas kernels  33.7 us (97%)
  local copies, waits for them, and re-layouts  0.88 us (3%)
    pallas_call x1, Pallas kernels, shards(): pl.pallas_call(functools.partial(kernel, sizes), out_shape=jax.ShapeDtype...  33.7 us
    unnamed x1, local copies, waits for them, and re-layouts  0.88 us

profile of v3, /device:TPU:1, one launch (start us, length us, event | category | flops | bytes accessed | tf_op | source)
XLA Modules:
  0.0 34.6 jit_solution(8032324498676219142)
XLA Ops:
  0.0 33.7 %shard_map.91 = f32[3,512,128]{2,1,0:T(8,128)S(1)} custom-call(f32[3,512,128]{2,1,0:T(8,128)} %bitcast.5, f32[2,8]{1,0:T(2,128)} %bitcast.6, f32[2,8]{1,0:T(2,128)} %bitcast.7, bf16[384,256]{1,0:T(8,128)(2,1)} %constant.12.clone.zf_hbm, bf16[2,176,512]{2,1,0:T(8,128)(2,1)} %constant.13.clone.into_hbm, bf16[2,128,512]{2,1,0:T(8,128)(2,1)} %constant.14.clone.outof_hbm, ...), custom_call_target="tpu_custom_call" | custom-call | tf_op jit(solution)/shard_map/pallas_call | solution.py:548
  33.7 0.9 %copy.11 = f32[3,16,32,128]{3,2,1,0:T(8,128)} copy(f32[3,16,32,128]{3,2,1,0:T(8,128)S(1)} %bitcast.4) | data formatting | bytes 1572864
